TPU v7x, 32 devices: a whole 2x2x4 slice. The times are simulated.
32 devices in a mesh: loader: 32 (over z, y, x, core).
Axes of the slice: x: 2, y: 2, z: 4, core: 2. Of those that a mesh axis runs over, the one named last changes fastest.
Arguments:
- image_embed: bfloat16 [49152, 512], P('loader'), may hold values from -600 to 600
- text_embed: bfloat16 [49152, 512], P('loader'), may hold values from -600 to 600
- keep_mask: int32 [49152], P('loader'), may hold values from 0 to 1
Outputs:
- packed_pairs: bfloat16 [49152, 1024], P('loader')
- pair_scores: float32 [49152], P('loader')
All inputs are finite; a program needn't handle non-finite values.
Results may differ from a plain program's by a relative error of at most 0.002.
Values may be sent and summed in bfloat16 or wider, within the bound.
No kernel may reach another device: no remote copies, remote signals or barrier semaphores. Data moves between devices by JAX's collectives and lax.ppermute only.
A program may use at most 64 MiB of HBM per device.

v0:
```python
import functools

import jax
import jax.numpy as jnp
from jax import lax
from jax.experimental import pallas as pl
from jax.experimental.pallas import tpu as pltpu
from jax.sharding import PartitionSpec as P


epsilon = 1e-06
TILE = 16
BLOCK = 256
SPLITS = (3, 6)
APART = (False, True, False)
WINDOWS = ((768, 704), (896, 832), (768, 768, 512), (1024, 1024, 256))

SMEM = pl.BlockSpec(memory_space=pltpu.SMEM)
VMEM = pl.BlockSpec(memory_space=pltpu.VMEM)


def group_of(devices):
    return 2 ** (devices.bit_length() // 2)


def dealt(rank, member, group):
    turn = group * TILE
    return rank // turn * TILE + jnp.clip(rank % turn - member * TILE, 0, TILE)


def pack_block(base, counts, ahead, block_of, packed, out):
    group = out.shape[0]
    tiles = out.shape[1] // TILE * group
    reach = BLOCK + TILE
    packed[...] = jnp.zeros_like(packed)
    r = lax.broadcasted_iota(jnp.int32, (reach, BLOCK), 0)
    position = base % TILE
    for b, count in enumerate(counts):
        at = pl.multiple_of(position // TILE * TILE, TILE)
        chosen = (ahead[b : b + 1, :] + position % TILE == r).astype(jnp.float32).astype(jnp.bfloat16)
        part = jnp.dot(chosen, block_of(b), preferred_element_type=jnp.float32).astype(jnp.bfloat16)
        packed[pl.ds(at, TILE), :] += part[:TILE]
        packed[pl.ds(at + TILE, BLOCK), :] = part[TILE:]
        position += count
    lap = tiles * TILE
    packed[:TILE, :] += packed[lap : lap + TILE, :]
    first = base // TILE % tiles

    def turn(t, _):
        for member in range(group):
            tile = t * group + member - first
            tile = jnp.where(tile < 0, tile + tiles, tile)
            out[member, pl.ds(pl.multiple_of(t * TILE, TILE), TILE), :] = packed[
                pl.ds(pl.multiple_of(tile * TILE, TILE), TILE), :
            ]
        return 0

    lax.fori_loop(0, tiles // group, turn, 0)


def kept_ahead(marks_ref):
    r = lax.broadcasted_iota(jnp.int32, (BLOCK, BLOCK), 0)
    c = lax.broadcasted_iota(jnp.int32, (BLOCK, BLOCK), 1)
    triangle = (r < c).astype(jnp.float32).astype(jnp.bfloat16)
    marks = marks_ref[...]
    ahead = jnp.dot(marks.astype(jnp.float32).astype(jnp.bfloat16), triangle, preferred_element_type=jnp.float32)
    return jnp.where(marks == 1, ahead.astype(jnp.int32), -2 * BLOCK)


def count_kernel(marks_ref, counts_ref):
    counts_ref[...] = jnp.full(counts_ref.shape, jnp.sum(marks_ref[...]), jnp.int32)


def first_pack_kernel(columns, all_ref, sums_ref, marks_ref, x_ref, out, edges, packed):
    devices = all_ref.shape[0]

    def step(s, total):
        edges[s] = total
        return total + all_ref[s, 0]

    edges[devices] = lax.fori_loop(0, devices, step, jnp.int32(0), unroll=8)
    base = edges[lax.axis_index("loader")]
    counts = [sums_ref[b] for b in range(marks_ref.shape[0])]
    pack_block(
        base, counts, kept_ahead(marks_ref), lambda b: x_ref[b * BLOCK : (b + 1) * BLOCK, columns], packed, out
    )


def pack_kernel(pieces, edges, sums_ref, marks_ref, left_ref, right_ref, *rest):
    outs, packed = rest[: len(pieces)], rest[len(pieces) :]
    base = edges[lax.axis_index("loader")]
    counts = [sums_ref[b] for b in range(marks_ref.shape[0])]
    ahead = kept_ahead(marks_ref)
    for p, (low, high) in enumerate(pieces):
        width = left_ref.shape[1]

        def block_of(b):
            rows = slice(b * BLOCK, (b + 1) * BLOCK)
            parts = []
            if low < width:
                parts.append(left_ref[rows, low : min(high, width)])
            if high > width:
                parts.append(right_ref[rows, max(low, width) - width : high - width])
            return parts[0] if len(parts) == 1 else jnp.concatenate(parts, axis=1)

        pack_block(base, counts, ahead, block_of, packed[p], outs[p])


def copy_rows(low, high, source, source_tile, target, target_tile):
    width = target.shape[-1]

    def ends(t):
        at = pl.ds(pl.multiple_of(target_tile(t) * TILE, TILE), TILE)
        return at, source[pl.ds(pl.multiple_of(source_tile(t) * TILE, TILE), TILE), :]

    def edge(t):
        at, value = ends(t)
        row = t * TILE + lax.broadcasted_iota(jnp.int32, (TILE, width), 0)
        target[at, :] = jnp.where((row >= low) & (row < high), value, target[at, :])

    def inner(t, _):
        at, value = ends(t)
        target[at, :] = value
        return 0

    first, last = low // TILE, high // TILE

    @pl.when((high > low) & (low % TILE != 0))
    def _():
        edge(first)

    lax.fori_loop((low + TILE - 1) // TILE, last, inner, 0)

    @pl.when((high > low) & (high % TILE != 0) & ((first != last) | (low % TILE == 0)))
    def _():
        edge(last)


def window_kernel(edges, parts, window):
    group, share = parts.shape[0], parts.shape[1]
    me = lax.axis_index("loader")
    member, plane = me % group, me // group
    tiles = share // TILE
    start = edges[plane * group] // (group * TILE)
    end = (start * TILE) + window.shape[0]

    def step(other, _):
        source = plane * group + other
        low = dealt(edges[source], member, group)
        high = jnp.minimum(dealt(edges[source + 1], member, group), end)
        copy_rows(low, high, parts.at[other], lambda t: t % tiles, window, lambda t: t - start)
        return 0

    lax.fori_loop(0, group, step, 0)


def place_window(edges, apart, group, rows, window, target):
    me = lax.axis_index("loader")
    member, plane = me % group, me // group
    origin = plane + apart
    planes = (edges.shape[0] - 1) // group
    bounded = jnp.minimum(origin, planes - 1)
    ranks = edges[bounded * group]
    low = jnp.maximum(dealt(ranks, member, group), rows * plane)
    high = dealt(edges[(bounded + 1) * group], member, group)
    high = jnp.where(origin < planes, jnp.minimum(high, rows * (plane + 1)), low)
    start = ranks // (group * TILE)
    first = rows // TILE * plane
    copy_rows(low, high, window, lambda t: t - start, target, lambda t: t - first)


def place_own(edges, parts, target):
    group, share = parts.shape[0], parts.shape[1]
    rows = target.shape[0]
    me = lax.axis_index("loader")
    member, plane = me % group, me // group
    tiles = share // TILE
    first = rows // TILE * plane
    target[...] = jnp.zeros_like(target)

    def step(other, _):
        source = plane * group + other
        low = jnp.maximum(dealt(edges[source], member, group), rows * plane)
        high = jnp.minimum(dealt(edges[source + 1], member, group), rows * (plane + 1))
        copy_rows(low, high, parts.at[other], lambda t: t % tiles, target, lambda t: t - first)
        return 0

    lax.fori_loop(0, group, step, 0)


def assemble_kernel(edges, parts, *rest):
    windows, target = rest[:-1], rest[-1]
    place_own(edges, parts, target)
    for k, window in enumerate(windows):
        place_window(edges, k + 1, parts.shape[0], target.shape[0], window, target)


def assemble_apart_kernel(hops, edges, parts, *rest):
    windows, outs, target = rest[:hops], rest[hops:-1], rest[-1]
    assemble_kernel(edges, parts, *windows, target)
    group, share = parts.shape[0], parts.shape[1]
    member = lax.axis_index("loader") % group
    for k in range(group):
        chunk = jnp.bitwise_xor(member, k) * share
        outs[k][...] = target[pl.ds(pl.multiple_of(chunk, TILE), share), :]


def place_kernel(group, edges, apart_ref, window, held, target):
    target[...] = held[...]
    place_window(edges, apart_ref[0], group, target.shape[0], window, target)


def finish_kernel(apart, *rest):
    parts, (packed, scores) = rest[:-2], rest[-2:]
    group = packed.shape[0] // (parts[0].shape[-2])
    member = lax.axis_index("loader") % group
    turn, width = group * TILE, packed.shape[1] // 2
    r = lax.broadcasted_iota(jnp.int32, (turn, turn), 0)
    c = lax.broadcasted_iota(jnp.int32, (turn, turn), 1)

    def step(t, _):
        source = pl.ds(pl.multiple_of(t * TILE, TILE), TILE)
        column, index = 0, 0
        for split in apart:
            width_here = parts[index].shape[-1]
            for k in range(group):
                owner = jnp.bitwise_xor(member, k) if split else k
                at = pl.ds(pl.multiple_of(t * turn + owner * TILE, TILE), TILE)
                tile = parts[index + k][source, :] if split else parts[index][k, source, :]
                packed[at, column : column + width_here] = tile
            column += width_here
            index += group if split else 1
        rows = pl.ds(pl.multiple_of(t * turn, turn), turn)
        units = []
        for low in (0, width):
            values = packed[rows, low : low + width].astype(jnp.float32)
            scale = lax.rsqrt(jnp.sum(values * values, axis=1, keepdims=True) / width + epsilon)
            unit = (values * scale).astype(packed.dtype)
            packed[rows, low : low + width] = unit
            units.append(unit)
        products = lax.dot_general(*units, (((1,), (1,)), ((), ())), preferred_element_type=jnp.float32)
        own = jnp.where(r == c, products, 0.0)
        scores[pl.ds(t, 1), :] = jnp.sum(own, axis=0, keepdims=True) / width
        return 0

    lax.fori_loop(0, packed.shape[0] // turn, step, 0, unroll=2)


def window_class_kernel(group, classes, edges, class_ref):
    planes = (edges.shape[0] - 1) // group
    turn = group * TILE
    needed = []
    rows = classes[-1]
    for hop in range(1, planes):
        most = jnp.int32(0)
        for p in range(hop, planes):
            start = edges[p * group]
            end = jnp.minimum(edges[(p + 1) * group], group * rows * (p - hop + 1))
            length = ((end + turn - 1) // turn - start // turn) * TILE
            most = jnp.maximum(most, jnp.where(end > start, length, 0))
        needed.append(most)
    chosen = jnp.int32(len(classes) - 1)
    for index in reversed(range(len(classes) - 1)):
        fits = jnp.bool_(True)
        for hop in range(planes - 1):
            room = classes[index][hop] if hop < len(classes[index]) else 0
            fits = fits & (needed[hop] <= room)
        chosen = jnp.where(fits, jnp.int32(index), chosen)
    class_ref[0] = chosen


def all_counts_of(marks, devices):
    counts = pl.pallas_call(
        count_kernel,
        out_shape=jax.ShapeDtypeStruct((devices, 128), jnp.int32),
        in_specs=[VMEM],
        out_specs=VMEM,
        name="count",
    )(marks)
    return lax.all_to_all(counts, "loader", 0, 0, tiled=True)


def exchange(parts, devices):
    group = parts.shape[0]
    planes = [[first + k for k in range(group)] for first in range(0, devices, group)]
    return lax.all_to_all(parts, "loader", 0, 0, axis_index_groups=planes, tiled=True)


def exchange_apart(parts, devices):
    received = [parts[0]]
    for k in range(1, len(parts)):
        received.append(lax.ppermute(parts[k], "loader", [(i, i ^ k) for i in range(devices)]))
    return received


def shards(image_embed, text_embed, keep_mask):
    rows, width = image_embed.shape
    devices = lax.axis_size("loader")
    group = group_of(devices)
    planes = devices // group
    share = rows // group
    dtype = image_embed.dtype
    turn = group * TILE
    bounds = [0] + [width * 2 * s // 8 for s in SPLITS] + [2 * width]
    widths = [high - low for low, high in zip(bounds, bounds[1:])]

    marks = keep_mask.reshape(rows // BLOCK, BLOCK)
    sums = jnp.sum(marks, axis=1)
    counts = all_counts_of(keep_mask, devices)

    def parts_of(chunk):
        return jax.ShapeDtypeStruct((group, share, widths[chunk]), dtype)

    def staging(chunk):
        return pltpu.VMEM((rows + BLOCK + 2 * TILE, widths[chunk]), dtype)

    first, edges = pl.pallas_call(
        functools.partial(first_pack_kernel, slice(bounds[0], bounds[1])),
        out_shape=[parts_of(0), jax.ShapeDtypeStruct((devices + 1,), jnp.int32)],
        in_specs=[SMEM, SMEM, VMEM, VMEM],
        out_specs=[VMEM, SMEM],
        scratch_shapes=[staging(0)],
        name="pack_first",
    )(counts, sums, marks, image_embed)

    def pack_rest():
        later = range(1, len(widths))
        return pl.pallas_call(
            functools.partial(pack_kernel, [(bounds[c], bounds[c + 1]) for c in later]),
            out_shape=[parts_of(c) for c in later],
            in_specs=[SMEM, SMEM, VMEM, VMEM, VMEM],
            out_specs=[VMEM] * len(later),
            scratch_shapes=[staging(c) for c in later],
            cost_estimate=pl.CostEstimate(flops=2**31, bytes_accessed=8 * rows * width, transcendentals=0),
            name="pack_rest",
        )(edges, sums, marks, image_embed, text_embed)

    def window_of(parts, length):
        return pl.pallas_call(
            window_kernel,
            out_shape=jax.ShapeDtypeStruct((length, parts.shape[2]), dtype),
            in_specs=[SMEM, VMEM],
            out_specs=VMEM,
            cost_estimate=pl.CostEstimate(flops=2**30, bytes_accessed=2 * rows * width, transcendentals=0),
            name="window",
        )(edges, parts)

    def assemble(parts, windows):
        return pl.pallas_call(
            assemble_kernel,
            out_shape=jax.ShapeDtypeStruct((rows, parts.shape[2]), dtype),
            in_specs=[SMEM] + [VMEM] * (1 + len(windows)),
            out_specs=VMEM,
            cost_estimate=pl.CostEstimate(flops=2**30, bytes_accessed=4 * rows * width, transcendentals=0),
            name="assemble",
        )(edges, parts, *windows)

    def assemble_apart(parts, windows):
        return pl.pallas_call(
            functools.partial(assemble_apart_kernel, len(windows)),
            out_shape=[jax.ShapeDtypeStruct((share, parts.shape[2]), dtype)] * group,
            in_specs=[SMEM] + [VMEM] * (1 + len(windows)),
            out_specs=[VMEM] * group,
            scratch_shapes=[pltpu.VMEM((rows, parts.shape[2]), dtype)],
            cost_estimate=pl.CostEstimate(flops=2**30, bytes_accessed=4 * rows * width, transcendentals=0),
            name="assemble_apart",
        )(edges, parts, *windows)

    def down(window):
        return lax.ppermute(window, "loader", [(i, i - group) for i in range(group, devices)])

    def gather(held):
        return exchange(held.reshape(group, share, held.shape[1]), devices)

    def fixed(lengths):
        def run(received, packed):
            chunks = [received]
            done = []
            for chunk in range(len(widths)):
                window = window_of(chunks[chunk], lengths[0])
                if chunk + 1 < len(widths):
                    window, following = lax.optimization_barrier((window, packed[chunk]))
                    chunks.append(exchange(following, devices))
                windows = []
                for length in lengths:
                    window = down(window[:length])
                    windows.append(window)
                held = (assemble_apart if APART[chunk] else assemble)(chunks[chunk], windows)
                done += exchange_apart(held, devices) if APART[chunk] else [gather(held)]
            return done

        return run

    def general(received, packed):
        parts = jnp.concatenate([received] + [exchange(part, devices) for part in packed], axis=2)
        window = window_of(parts, rows + TILE)
        held = assemble(parts, [])

        def hop(k, state):
            window, held = state
            window = down(window)
            held = pl.pallas_call(
                functools.partial(place_kernel, group),
                out_shape=jax.ShapeDtypeStruct(held.shape, dtype),
                in_specs=[SMEM, SMEM, VMEM, VMEM],
                out_specs=VMEM,
                name="place",
            )(edges, k.reshape(1), window, held)
            return window, held

        _, held = lax.fori_loop(1, planes, hop, (window, held))
        held = gather(held)
        member = lax.axis_index("loader") % group
        done = []
        for split, low, high in zip(APART, bounds, bounds[1:]):
            if split:
                done += [
                    lax.dynamic_index_in_dim(held, member ^ k, 0, keepdims=False)[:, low:high] for k in range(group)
                ]
            else:
                done.append(held[:, :, low:high])
        return done

    lengths = [w for w in WINDOWS if w[0] <= rows and len(w) < planes]
    chosen = pl.pallas_call(
        functools.partial(window_class_kernel, group, tuple(lengths) + (rows,)),
        out_shape=jax.ShapeDtypeStruct((1,), jnp.int32),
        in_specs=[SMEM],
        out_specs=SMEM,
        name="choose",
    )(edges)
    received = exchange(first, devices)
    branches = [fixed(w) for w in lengths] + [general]
    done = lax.switch(chosen[0], branches, received, pack_rest())
    packed_pairs, scores = pl.pallas_call(
        functools.partial(finish_kernel, APART),
        out_shape=[
            jax.ShapeDtypeStruct((rows, 2 * width), dtype),
            jax.ShapeDtypeStruct((rows // turn, turn), jnp.float32),
        ],
        in_specs=[VMEM] * len(done),
        out_specs=[VMEM] * 2,
        name="finish",
    )(*done)
    return packed_pairs, scores.reshape(rows)


def solution(mesh):
    placed = (P("loader", None), P("loader", None), P("loader"))
    return jax.shard_map(
        shards,
        mesh=mesh,
        in_specs=placed,
        out_specs=(P("loader", None), P("loader")),
        check_vma=False,
    )
```

profile of v0, /device:TPU:0, one launch (start us, length us, event | category | flops | bytes accessed | tf_op | source)
XLA Modules:
  0.0 186.2 jit_solution(12449043123649447654)
XLA Ops:
  0.6 1.4 count.1
  2.1 7.3 %all-to-all-start.19 = ((s32[32,1,128]{2,1,0:T(1,128)}), s32[32,1,128]{2,1,0:T(1,128)S(1)}, u32[]{:S(2)}, u32[]{:S(2)}) async-start(s32[32,1,128]{2,1,0:T(1,128)} %bitcast.44), calls=%async_computation.19 | async-start | bytes 32768 | tf_op jit(solution)/shard_map/all_to_all | solution.py:280
  10.7 5.8 %all-to-all-done.19 = s32[32,1,128]{2,1,0:T(1,128)S(1)} async-done(((s32[32,1,128]{2,1,0:T(1,128)}), s32[32,1,128]{2,1,0:T(1,128)S(1)}, u32[]{:S(2)}, u32[]{:S(2)}) %all-to-all-start.19) | async-done | bytes 16416 | tf_op jit(solution)/shard_map/all_to_all | solution.py:280
  17.1 3.7 %pack_first.1 = (bf16[8,192,384]{2,1,0:T(8,128)(2,1)}, s32[33]{0:T(128)S(1)}) custom-call(s32[32,128]{1,0:T(8,128)} %bitcast.43, s32[6]{0:T(128)} %reduce_sum.9.sums_ref, s32[6,256]{1,0:T(8,128)} %copy-done.22, bf16[1536,512]{1,0:T(8,128)(2,1)} %left_ref.1), custom_call_target="tpu_custom_call" | custom-call | tf_op jit(solution)/shard_map/pack_first/pallas_call | solution.py:317
  20.8 3.6 %all-to-all-start.20 = ((bf16[8,192,384]{2,1,0:T(8,128)(2,1)}), bf16[8,192,384]{2,1,0:T(8,128)(2,1)S(1)}, u32[]{:S(2)}, u32[]{:S(2)}) async-start(bf16[8,192,384]{2,1,0:T(8,128)(2,1)} %get-tuple-element.201), calls=%async_computation.20 | async-start | bytes 2359296 | tf_op jit(solution)/shard_map/all_to_all | solution.py:286
  24.4 1.1 choose.1
  26.0 5.2 %pack_rest.1 = (bf16[8,192,384]{2,1,0:T(8,128)(2,1)}, bf16[8,192,256]{2,1,0:T(8,128)(2,1)}) custom-call(s32[33]{0:T(128)S(1)} %get-tuple-element.200.edges, s32[6]{0:T(128)} %reduce_sum.9.sums_ref, s32[6,256]{1,0:T(8,128)} %copy-done.22, bf16[1536,512]{1,0:T(8,128)(2,1)} %left_ref.1, bf16[1536,512]{1,0:T(8,128)(2,1)} %right_ref.1), custom_call_target="tpu_custom_call" | custom-call | flops 2147483648 | bytes 6291456 | tf_op jit(solution)/shard_map/pack_rest/pallas_call | solution.py:328
  31.2 9.9 %all-to-all-done.20 = bf16[8,192,384]{2,1,0:T(8,128)(2,1)S(1)} async-done(((bf16[8,192,384]{2,1,0:T(8,128)(2,1)}), bf16[8,192,384]{2,1,0:T(8,128)(2,1)S(1)}, u32[]{:S(2)}, u32[]{:S(2)}) %all-to-all-start.20) | async-done | bytes 1179680 | tf_op jit(solution)/shard_map/all_to_all | solution.py:286
  41.1 138.7 %conditional.1 = (bf16[8,192,384]{2,1,0:T(8,128)(2,1)}, bf16[192,384]{1,0:T(8,128)(2,1)S(1)}, bf16[192,384]{1,0:T(8,128)(2,1)}, bf16[192,384]{1,0:T(8,128)(2,1)}...) conditional(s32[]{:T(128)} %bitcast.21, (s32[33]{0:T(128)S(1)}, ...), branch_computations={%region_1.0_spmd, %region_2.0_spmd, %region_3.0_spmd, %region_4.0_... | conditional | flops 6442450944 | bytes 97846176 | solution.py:434
  41.1 2.1 %window.19 = bf16[768,384]{1,0:T(8,128)(2,1)} custom-call(s32[33]{0:T(128)S(1)} %get-tuple-element.140.edges, bf16[8,192,384]{2,1,0:T(8,128)(2,1)S(1)} %get-tuple-element.141.parts), custom_call_target="tpu_custom_call" | custom-call | flops 1073741824 | bytes 1572864 | tf_op jit(solution)/shard_map/cond/branch_2_fun/window/pallas_call | solution.py:339
  43.2 3.6 %all-to-all-start.9 = ((bf16[8,192,384]{2,1,0:T(8,128)(2,1)}), bf16[8,192,384]{2,1,0:T(8,128)(2,1)S(1)}, u32[]{:S(2)}, u32[]{:S(2)}) async-start(bf16[8,192,384]{2,1,0:T(8,128)(2,1)} %get-tuple-element.144), calls=%async_computation.9 | async-start | bytes 2359296 | tf_op jit(solution)/shard_map/cond/branch_2_fun/all_to_all | solution.py:286
  46.8 1.3 collective-permute-start.26
  48.1 16.5 %collective-permute-done.26.rest_0_ = bf16[768,384]{1,0:T(8,128)(2,1)} collective-permute-done((bf16[768,384]{1,0:T(8,128)(2,1)}, bf16[768,384]{1,0:T(8,128)(2,1)}, u32[]{:S(2)}, u32[]{:S(2)}) %collective-permute-start.26) | collective-permute-done | bytes 589856 | tf_op jit(solution)/shard_map/cond/branch_2_fun/ppermute | solution.py:370
  64.6 1.3 collective-permute-start.27
  65.9 1.0 copy-done.5
  66.9 2.9 %window.20 = bf16[768,384]{1,0:T(8,128)(2,1)} custom-call(s32[33]{0:T(128)S(1)} %get-tuple-element.140.edges, bf16[8,192,384]{2,1,0:T(8,128)(2,1)} %copy-done.5), custom_call_target="tpu_custom_call" | custom-call | flops 1073741824 | bytes 1572864 | tf_op jit(solution)/shard_map/cond/branch_2_fun/window/pallas_call | solution.py:339
  69.8 3.9 %all-to-all-start.10 = ((bf16[8,192,256]{2,1,0:T(8,128)(2,1)}), bf16[8,192,256]{2,1,0:T(8,128)(2,1)S(1)}, u32[]{:S(2)}, u32[]{:S(2)}) async-start(bf16[8,192,256]{2,1,0:T(8,128)(2,1)} %get-tuple-element.155), calls=%async_computation.10 | async-start | bytes 1572864 | tf_op jit(solution)/shard_map/cond/branch_2_fun/all_to_all | solution.py:286
  73.6 7.8 %collective-permute-done.27.rest_1_ = bf16[768,384]{1,0:T(8,128)(2,1)S(1)} collective-permute-done((bf16[768,384]{1,0:T(8,128)(2,1)}, bf16[768,384]{1,0:T(8,128)(2,1)S(1)}, u32[]{:S(2)}, u32[]{:S(2)}) %collective-permute-start.27) | collective-permute-done | bytes 589856 | tf_op jit(solution)/shard_map/cond/branch_2_fun/ppermute | solution.py:370
  81.5 1.3 collective-permute-start.28
  82.8 1.3 collective-permute-start.29
  84.1 2.1 %all-to-all-done.10.parts = bf16[8,192,256]{2,1,0:T(8,128)(2,1)S(1)} async-done(((bf16[8,192,256]{2,1,0:T(8,128)(2,1)}), bf16[8,192,256]{2,1,0:T(8,128)(2,1)S(1)}, u32[]{:S(2)}, u32[]{:S(2)}) %all-to-all-start.10) | async-done | bytes 786464 | tf_op jit(solution)/shard_map/cond/branch_2_fun/all_to_all | solution.py:286
  86.2 0.9 copy-done.9
  87.1 2.6 %window.21 = bf16[768,256]{1,0:T(8,128)(2,1)} custom-call(s32[33]{0:T(128)S(1)} %get-tuple-element.140.edges, bf16[8,192,256]{2,1,0:T(8,128)(2,1)} %copy-done.9), custom_call_target="tpu_custom_call" | custom-call | flops 1073741824 | bytes 1572864 | tf_op jit(solution)/shard_map/cond/branch_2_fun/window/pallas_call | solution.py:339
  89.8 1.3 collective-permute-start.39
  91.1 4.5 %collective-permute-done.28.rest_2_ = bf16[512,384]{1,0:T(8,128)(2,1)} collective-permute-done((bf16[512,384]{1,0:T(8,128)(2,1)S(1)}, bf16[512,384]{1,0:T(8,128)(2,1)}, u32[]{:S(2)}, u32[]{:S(2)}) %collective-permute-start.28) | collective-permute-done | bytes 393248 | tf_op jit(solution)/shard_map/cond/branch_2_fun/ppermute | solution.py:370
  95.5 3.9 %assemble.13 = bf16[1536,384]{1,0:T(8,128)(2,1)} custom-call(s32[33]{0:T(128)S(1)} %get-tuple-element.140.edges, bf16[8,192,384]{2,1,0:T(8,128)(2,1)S(1)} %get-tuple-element.141.parts, bf16[768,384]{1,0:T(8,128)(2,1)} %collective-permute-done.26.rest_0_, bf16[768,384]{1,0:T(8,128)(2,1)} %copy-done.19, bf16[512,384]{1,0:T(8,128)(2,1)} %collective-permute-done.28.rest_2_), custom_call_target="tpu_custom_call" | custom-call | flops 1073741824 | bytes 3145728 | tf_op jit(solution)/shard_map/cond/branch_2_fun/assemble/pallas_call | solution.py:349
  99.4 4.3 %all-to-all-start.8 = ((bf16[8,192,384]{2,1,0:T(8,128)(2,1)}), bf16[8,192,384]{2,1,0:T(8,128)(2,1)}, u32[]{:S(2)}, u32[]{:S(2)}) async-start(bf16[8,192,384]{2,1,0:T(8,128)(2,1)} %bitcast.36), calls=%async_computation.8 | async-start | bytes 2359296 | tf_op jit(solution)/shard_map/cond/branch_2_fun/all_to_all | solution.py:286
  103.7 10.5 %collective-permute-done.39.rest_0_ = bf16[768,256]{1,0:T(8,128)(2,1)S(1)} collective-permute-done((bf16[768,256]{1,0:T(8,128)(2,1)}, bf16[768,256]{1,0:T(8,128)(2,1)S(1)}, u32[]{:S(2)}, u32[]{:S(2)}) %collective-permute-start.39) | collective-permute-done | bytes 393248 | tf_op jit(solution)/shard_map/cond/branch_2_fun/ppermute | solution.py:370
  114.2 1.3 collective-permute-start.40
  115.5 1.3 collective-permute-start.30
  116.8 11.3 %collective-permute-done.40.rest_1_ = bf16[768,256]{1,0:T(8,128)(2,1)S(1)} collective-permute-done((bf16[768,256]{1,0:T(8,128)(2,1)S(1)}, bf16[768,256]{1,0:T(8,128)(2,1)S(1)}, u32[]{:S(2)}, u32[]{:S(2)}) %collective-permute-start.40) | collective-permute-done | bytes 393248 | tf_op jit(solution)/shard_map/cond/branch_2_fun/ppermute | solution.py:370
  128.1 1.3 collective-permute-start.41
  129.4 11.3 %collective-permute-done.30.rest_1_ = bf16[768,384]{1,0:T(8,128)(2,1)S(1)} collective-permute-done((bf16[768,384]{1,0:T(8,128)(2,1)}, bf16[768,384]{1,0:T(8,128)(2,1)S(1)}, u32[]{:S(2)}, u32[]{:S(2)}) %collective-permute-start.30) | collective-permute-done | bytes 589856 | tf_op jit(solution)/shard_map/cond/branch_2_fun/ppermute | solution.py:370
  140.7 1.3 collective-permute-start.31
  142.0 4.3 %collective-permute-done.41.rest_2_ = bf16[512,256]{1,0:T(8,128)(2,1)S(1)} collective-permute-done((bf16[512,256]{1,0:T(8,128)(2,1)S(1)}, bf16[512,256]{1,0:T(8,128)(2,1)S(1)}, u32[]{:S(2)}, u32[]{:S(2)}) %collective-permute-start.41) | collective-permute-done | bytes 262176 | tf_op jit(solution)/shard_map/cond/branch_2_fun/ppermute | solution.py:370
  146.3 0.7 copy-done.34
  147.1 3.8 %assemble.14 = bf16[1536,256]{1,0:T(8,128)(2,1)} custom-call(s32[33]{0:T(128)S(1)} %get-tuple-element.140.edges, bf16[8,192,256]{2,1,0:T(8,128)(2,1)} %copy-done.9, bf16[768,256]{1,0:T(8,128)(2,1)} %copy-done.31, bf16[768,256]{1,0:T(8,128)(2,1)} %copy-done.21, bf16[512,256]{1,0:T(8,128)(2,1)} %copy-done.34), custom_call_target="tpu_custom_call" | custom-call | flops 1073741824 | bytes 3145728 | tf_op jit(solution)/shard_map/cond/branch_2_fun/assemble/pallas_call | solution.py:349
  150.8 4.2 %all-to-all-start.11 = ((bf16[8,192,256]{2,1,0:T(8,128)(2,1)}), bf16[8,192,256]{2,1,0:T(8,128)(2,1)}, u32[]{:S(2)}, u32[]{:S(2)}) async-start(bf16[8,192,256]{2,1,0:T(8,128)(2,1)} %bitcast.40), calls=%async_computation.11 | async-start | bytes 1572864 | tf_op jit(solution)/shard_map/cond/branch_2_fun/all_to_all | solution.py:286
  155.8 4.4 %assemble_apart.6 = (bf16[192,384]{1,0:T(8,128)(2,1)S(1)}, bf16[192,384]{1,0:T(8,128)(2,1)}, bf16[192,384]{1,0:T(8,128)(2,1)}, bf16[192,384]{1,0:T(8,128)(2,1)},...) custom-call(s32[33]{0:T(128)S(1)} %get-tuple-element.140.edges, ...), custom_call_target="tpu_custom_call" | custom-call | flops 1073741824 | bytes 3145728 | tf_op jit(solution)/shard_map/cond/branch_2_fun/assemble_apart/pallas_call | solution.py:359
  160.6 1.6 collective-permute-start.33
  162.2 1.7 collective-permute-start.35
  164.0 2.6 %collective-permute-start.37 = (bf16[192,384]{1,0:T(8,128)(2,1)}, bf16[192,384]{1,0:T(8,128)(2,1)}, u32[]{:S(2)}, u32[]{:S(2)}) collective-permute-start(bf16[192,384]{1,0:T(8,128)(2,1)} %get-tuple-element.153), channel_id=1, source_target_pairs={{0,6},{1,7},{2,4},{3,5},{4,2},{5,3},{6,0},{7,1},{8,14},{9,15},{10,... | collective-permute-start | bytes 442376 | tf_op jit(solution)/shard_map/cond/branch_2_fun/ppermute | solution.py:292
  166.6 3.8 %collective-permute-done.33 = bf16[192,384]{1,0:T(8,128)(2,1)} collective-permute-done((bf16[192,384]{1,0:T(8,128)(2,1)}, bf16[192,384]{1,0:T(8,128)(2,1)}, u32[]{:S(2)}, u32[]{:S(2)}) %collective-permute-start.33) | collective-permute-done | bytes 147488 | tf_op jit(solution)/shard_map/cond/branch_2_fun/ppermute | solution.py:292
  170.5 2.0 %collective-permute-done.34 = bf16[192,384]{1,0:T(8,128)(2,1)} collective-permute-done((bf16[192,384]{1,0:T(8,128)(2,1)}, bf16[192,384]{1,0:T(8,128)(2,1)}, u32[]{:S(2)}, u32[]{:S(2)}) %collective-permute-start.34) | collective-permute-done | bytes 147488 | tf_op jit(solution)/shard_map/cond/branch_2_fun/ppermute | solution.py:292
  172.4 1.1 collective-permute-done.36
  173.5 4.2 %collective-permute-done.37 = bf16[192,384]{1,0:T(8,128)(2,1)} collective-permute-done((bf16[192,384]{1,0:T(8,128)(2,1)}, bf16[192,384]{1,0:T(8,128)(2,1)}, u32[]{:S(2)}, u32[]{:S(2)}) %collective-permute-start.37) | collective-permute-done | bytes 147488 | tf_op jit(solution)/shard_map/cond/branch_2_fun/ppermute | solution.py:292
  177.7 2.0 %collective-permute-done.38 = bf16[192,384]{1,0:T(8,128)(2,1)} collective-permute-done((bf16[192,384]{1,0:T(8,128)(2,1)}, bf16[192,384]{1,0:T(8,128)(2,1)}, u32[]{:S(2)}, u32[]{:S(2)}) %collective-permute-start.38) | collective-permute-done | bytes 147488 | tf_op jit(solution)/shard_map/cond/branch_2_fun/ppermute | solution.py:292
  179.7 6.5 %finish.1 = (bf16[1536,1024]{1,0:T(8,128)(2,1)}, f32[12,128]{1,0:T(8,128)}) custom-call(bf16[8,192,384]{2,1,0:T(8,128)(2,1)} %get-tuple-element.204.rest_0_, bf16[192,384]{1,0:T(8,128)(2,1)S(1)} %get-tuple-element.205.rest_1_, bf16[192,384]{1,0:T(8,128)(2,1)} %get-tuple-element.206.rest_2_, bf16[192,384]{1,0:T(8,128)(2,1)} %get-tuple-element.207.rest_3_, ...), custom_call_target="tpu_custom_call" | custom-call | tf_op jit(solution)/shard_map/finish/pallas_call | solution.py:435
  (33 shorter events, 3.4 us)
Async XLA Ops:
  2.1 14.4 %all-to-all-start.19 = ((s32[32,1,128]{2,1,0:T(1,128)}), s32[32,1,128]{2,1,0:T(1,128)S(1)}, u32[]{:S(2)}, u32[]{:S(2)}) async-start(s32[32,1,128]{2,1,0:T(1,128)} %bitcast.44), calls=%async_computation.19 | async-start | bytes 32768 | tf_op jit(solution)/shard_map/all_to_all | solution.py:280
  10.1 6.4 %copy-start.22 = (s32[6,256]{1,0:T(8,128)}, s32[6,256]{1,0:T(8,128)S(1)}, u32[]{:S(2)}) copy-start(s32[6,256]{1,0:T(8,128)S(1)} %reshape.45.marks_ref) | copy-start | bytes 18436
  16.5 0.6 copy-start.23
  20.8 20.3 %all-to-all-start.20 = ((bf16[8,192,384]{2,1,0:T(8,128)(2,1)}), bf16[8,192,384]{2,1,0:T(8,128)(2,1)S(1)}, u32[]{:S(2)}, u32[]{:S(2)}) async-start(bf16[8,192,384]{2,1,0:T(8,128)(2,1)} %get-tuple-element.201), calls=%async_computation.20 | async-start | bytes 2359296 | tf_op jit(solution)/shard_map/all_to_all | solution.py:286
  43.2 22.7 %all-to-all-start.9 = ((bf16[8,192,384]{2,1,0:T(8,128)(2,1)}), bf16[8,192,384]{2,1,0:T(8,128)(2,1)S(1)}, u32[]{:S(2)}, u32[]{:S(2)}) async-start(bf16[8,192,384]{2,1,0:T(8,128)(2,1)} %get-tuple-element.144), calls=%async_computation.9 | async-start | bytes 2359296 | tf_op jit(solution)/shard_map/cond/branch_2_fun/all_to_all | solution.py:286
  46.8 17.8 %collective-permute-start.26 = (bf16[768,384]{1,0:T(8,128)(2,1)}, bf16[768,384]{1,0:T(8,128)(2,1)}, u32[]{:S(2)}, u32[]{:S(2)}) collective-permute-start(bf16[768,384]{1,0:T(8,128)(2,1)} %window.19), channel_id=1, source_target_pairs={{8,0},{9,1},{10,2},{11,3},{12,4},{13,5},{14,6},{15,7},{16,8},{17,9... | collective-permute-start | bytes 1769480 | tf_op jit(solution)/shard_map/cond/branch_2_fun/ppermute | solution.py:370
  64.6 16.9 %collective-permute-start.27 = (bf16[768,384]{1,0:T(8,128)(2,1)}, bf16[768,384]{1,0:T(8,128)(2,1)S(1)}, u32[]{:S(2)}, u32[]{:S(2)}) collective-permute-start(bf16[768,384]{1,0:T(8,128)(2,1)} %collective-permute-done.26.rest_0_), channel_id=1, source_target_pairs={{8,0},{9,1},{10,2},{11,3},{12,4},{13,5},{14,6},{15,7},{16,8},{17,9... | collective-permute-start | bytes 1769480 | tf_op jit(solution)/shard_map/cond/branch_2_fun/ppermute | solution.py:370
  65.9 1.0 copy-start.5
  69.8 16.4 %all-to-all-start.10 = ((bf16[8,192,256]{2,1,0:T(8,128)(2,1)}), bf16[8,192,256]{2,1,0:T(8,128)(2,1)S(1)}, u32[]{:S(2)}, u32[]{:S(2)}) async-start(bf16[8,192,256]{2,1,0:T(8,128)(2,1)} %get-tuple-element.155), calls=%async_computation.10 | async-start | bytes 1572864 | tf_op jit(solution)/shard_map/cond/branch_2_fun/all_to_all | solution.py:286
  81.5 14.0 %copy-start.19 = (bf16[768,384]{1,0:T(8,128)(2,1)}, bf16[768,384]{1,0:T(8,128)(2,1)S(1)}, u32[]{:S(2)}) copy-start(bf16[768,384]{1,0:T(8,128)(2,1)S(1)} %collective-permute-done.27.rest_1_) | copy-start | bytes 1769476 | tf_op jit(solution)/shard_map/cond
  81.5 14.0 %collective-permute-start.28 = (bf16[512,384]{1,0:T(8,128)(2,1)S(1)}, bf16[512,384]{1,0:T(8,128)(2,1)}, u32[]{:S(2)}, u32[]{:S(2)}) collective-permute-start(bf16[512,384]{1,0:T(8,128)(2,1)S(1)} %slice.72), channel_id=1, source_target_pairs={{8,0},{9,1},{10,2},{11,3},{12,4},{13,5},{14,6},{15,7},{16,8},{17,9... | collective-permute-start | bytes 1179656 | tf_op jit(solution)/shard_map/cond/branch_2_fun/ppermute | solution.py:370
  82.8 32.7 %collective-permute-start.29 = (bf16[768,384]{1,0:T(8,128)(2,1)}, bf16[768,384]{1,0:T(8,128)(2,1)}, u32[]{:S(2)}, u32[]{:S(2)}) collective-permute-start(bf16[768,384]{1,0:T(8,128)(2,1)} %window.20), channel_id=1, source_target_pairs={{8,0},{9,1},{10,2},{11,3},{12,4},{13,5},{14,6},{15,7},{16,8},{17,9... | collective-permute-start | bytes 1769480 | tf_op jit(solution)/shard_map/cond/branch_2_fun/ppermute | solution.py:370
  86.2 0.9 copy-start.9
  89.8 24.4 %collective-permute-start.39 = (bf16[768,256]{1,0:T(8,128)(2,1)}, bf16[768,256]{1,0:T(8,128)(2,1)S(1)}, u32[]{:S(2)}, u32[]{:S(2)}) collective-permute-start(bf16[768,256]{1,0:T(8,128)(2,1)} %window.21), channel_id=1, source_target_pairs={{8,0},{9,1},{10,2},{11,3},{12,4},{13,5},{14,6},{15,7},{16,8},{17,9... | collective-permute-start | bytes 1179656 | tf_op jit(solution)/shard_map/cond/branch_2_fun/ppermute | solution.py:370
  99.4 51.4 %all-to-all-start.8 = ((bf16[8,192,384]{2,1,0:T(8,128)(2,1)}), bf16[8,192,384]{2,1,0:T(8,128)(2,1)}, u32[]{:S(2)}, u32[]{:S(2)}) async-start(bf16[8,192,384]{2,1,0:T(8,128)(2,1)} %bitcast.36), calls=%async_computation.8 | async-start | bytes 2359296 | tf_op jit(solution)/shard_map/cond/branch_2_fun/all_to_all | solution.py:286
  114.2 32.1 %copy-start.31 = (bf16[768,256]{1,0:T(8,128)(2,1)}, bf16[768,256]{1,0:T(8,128)(2,1)S(1)}, u32[]{:S(2)}) copy-start(bf16[768,256]{1,0:T(8,128)(2,1)S(1)} %collective-permute-done.39.rest_0_) | copy-start | bytes 1179652 | tf_op jit(solution)/shard_map/cond
  114.2 13.9 %collective-permute-start.40 = (bf16[768,256]{1,0:T(8,128)(2,1)S(1)}, bf16[768,256]{1,0:T(8,128)(2,1)S(1)}, u32[]{:S(2)}, u32[]{:S(2)}) collective-permute-start(bf16[768,256]{1,0:T(8,128)(2,1)S(1)} %collective-permute-done.39.rest_0_), channel_id=1, source_target_pairs={{8,0},{9,1},{10,2},{11,3},{12,4},{13,5},{14,6},{15,7},{16,8},{17,9... | collective-permute-start | bytes 1179656 | tf_op jit(solution)/shard_map/cond/branch_2_fun/ppermute | solution.py:370
  115.5 25.2 %collective-permute-start.30 = (bf16[768,384]{1,0:T(8,128)(2,1)}, bf16[768,384]{1,0:T(8,128)(2,1)S(1)}, u32[]{:S(2)}, u32[]{:S(2)}) collective-permute-start(bf16[768,384]{1,0:T(8,128)(2,1)} %collective-permute-done.29.rest_0_), channel_id=1, source_target_pairs={{8,0},{9,1},{10,2},{11,3},{12,4},{13,5},{14,6},{15,7},{16,8},{17,9... | collective-permute-start | bytes 1769480 | tf_op jit(solution)/shard_map/cond/branch_2_fun/ppermute | solution.py:370
  128.0 18.3 %copy-start.21 = (bf16[768,256]{1,0:T(8,128)(2,1)}, bf16[768,256]{1,0:T(8,128)(2,1)S(1)}, u32[]{:S(2)}) copy-start(bf16[768,256]{1,0:T(8,128)(2,1)S(1)} %collective-permute-done.40.rest_1_) | copy-start | bytes 1179652 | tf_op jit(solution)/shard_map/cond
  128.1 18.2 %collective-permute-start.41 = (bf16[512,256]{1,0:T(8,128)(2,1)S(1)}, bf16[512,256]{1,0:T(8,128)(2,1)S(1)}, u32[]{:S(2)}, u32[]{:S(2)}) collective-permute-start(bf16[512,256]{1,0:T(8,128)(2,1)S(1)} %slice.74), channel_id=1, source_target_pairs={{8,0},{9,1},{10,2},{11,3},{12,4},{13,5},{14,6},{15,7},{16,8},{17,9... | collective-permute-start | bytes 786440 | tf_op jit(solution)/shard_map/cond/branch_2_fun/ppermute | solution.py:370
  140.7 10.1 %copy-start.18 = (bf16[768,384]{1,0:T(8,128)(2,1)}, bf16[768,384]{1,0:T(8,128)(2,1)S(1)}, u32[]{:S(2)}) copy-start(bf16[768,384]{1,0:T(8,128)(2,1)S(1)} %collective-permute-done.30.rest_1_) | copy-start | bytes 1769476 | tf_op jit(solution)/shard_map/cond
  140.7 14.3 %collective-permute-start.31 = (bf16[512,384]{1,0:T(8,128)(2,1)S(1)}, bf16[512,384]{1,0:T(8,128)(2,1)S(1)}, u32[]{:S(2)}, u32[]{:S(2)}) collective-permute-start(bf16[512,384]{1,0:T(8,128)(2,1)S(1)} %slice.73), channel_id=1, source_target_pairs={{8,0},{9,1},{10,2},{11,3},{12,4},{13,5},{14,6},{15,7},{16,8},{17,9... | collective-permute-start | bytes 1179656 | tf_op jit(solution)/shard_map/cond/branch_2_fun/ppermute | solution.py:370
  146.3 0.7 copy-start.34
  150.8 28.9 %all-to-all-start.11 = ((bf16[8,192,256]{2,1,0:T(8,128)(2,1)}), bf16[8,192,256]{2,1,0:T(8,128)(2,1)}, u32[]{:S(2)}, u32[]{:S(2)}) async-start(bf16[8,192,256]{2,1,0:T(8,128)(2,1)} %bitcast.40), calls=%async_computation.11 | async-start | bytes 1572864 | tf_op jit(solution)/shard_map/cond/branch_2_fun/all_to_all | solution.py:286
  155.0 0.7 copy-start.32
  160.2 3.9 %collective-permute-start.32 = (bf16[192,384]{1,0:T(8,128)(2,1)}, bf16[192,384]{1,0:T(8,128)(2,1)}, u32[]{:S(2)}, u32[]{:S(2)}) collective-permute-start(bf16[192,384]{1,0:T(8,128)(2,1)} %get-tuple-element.148), channel_id=1, source_target_pairs={{0,1},{1,0},{2,3},{3,2},{4,5},{5,4},{6,7},{7,6},{8,9},{9,8},{10,11... | collective-permute-start | bytes 442376 | tf_op jit(solution)/shard_map/cond/branch_2_fun/ppermute | solution.py:292
  160.6 9.9 %collective-permute-start.33 = (bf16[192,384]{1,0:T(8,128)(2,1)}, bf16[192,384]{1,0:T(8,128)(2,1)}, u32[]{:S(2)}, u32[]{:S(2)}) collective-permute-start(bf16[192,384]{1,0:T(8,128)(2,1)} %get-tuple-element.149), channel_id=1, source_target_pairs={{0,2},{1,3},{2,0},{3,1},{4,6},{5,7},{6,4},{7,5},{8,10},{9,11},{10,... | collective-permute-start | bytes 442376 | tf_op jit(solution)/shard_map/cond/branch_2_fun/ppermute | solution.py:292
  162.2 10.3 %collective-permute-start.34 = (bf16[192,384]{1,0:T(8,128)(2,1)}, bf16[192,384]{1,0:T(8,128)(2,1)}, u32[]{:S(2)}, u32[]{:S(2)}) collective-permute-start(bf16[192,384]{1,0:T(8,128)(2,1)} %get-tuple-element.150), channel_id=1, source_target_pairs={{0,3},{1,2},{2,1},{3,0},{4,7},{5,6},{6,5},{7,4},{8,11},{9,10},{10,... | collective-permute-start | bytes 442376 | tf_op jit(solution)/shard_map/cond/branch_2_fun/ppermute | solution.py:292
  162.2 10.3 %collective-permute-start.35 = (bf16[192,384]{1,0:T(8,128)(2,1)}, bf16[192,384]{1,0:T(8,128)(2,1)}, u32[]{:S(2)}, u32[]{:S(2)}) collective-permute-start(bf16[192,384]{1,0:T(8,128)(2,1)} %get-tuple-element.151), channel_id=1, source_target_pairs={{0,4},{1,5},{2,6},{3,7},{4,0},{5,1},{6,2},{7,3},{8,12},{9,13},{10,... | collective-permute-start | bytes 442376 | tf_op jit(solution)/shard_map/cond/branch_2_fun/ppermute | solution.py:292
  163.9 9.6 %collective-permute-start.36 = (bf16[192,384]{1,0:T(8,128)(2,1)}, bf16[192,384]{1,0:T(8,128)(2,1)}, u32[]{:S(2)}, u32[]{:S(2)}) collective-permute-start(bf16[192,384]{1,0:T(8,128)(2,1)} %get-tuple-element.152), channel_id=1, source_target_pairs={{0,5},{1,4},{2,7},{3,6},{4,1},{5,0},{6,3},{7,2},{8,13},{9,12},{10,... | collective-permute-start | bytes 442376 | tf_op jit(solution)/shard_map/cond/branch_2_fun/ppermute | solution.py:292
  164.0 13.7 %collective-permute-start.37 = (bf16[192,384]{1,0:T(8,128)(2,1)}, bf16[192,384]{1,0:T(8,128)(2,1)}, u32[]{:S(2)}, u32[]{:S(2)}) collective-permute-start(bf16[192,384]{1,0:T(8,128)(2,1)} %get-tuple-element.153), channel_id=1, source_target_pairs={{0,6},{1,7},{2,4},{3,5},{4,2},{5,3},{6,0},{7,1},{8,14},{9,15},{10,... | collective-permute-start | bytes 442376 | tf_op jit(solution)/shard_map/cond/branch_2_fun/ppermute | solution.py:292
  170.4 9.3 %collective-permute-start.38 = (bf16[192,384]{1,0:T(8,128)(2,1)}, bf16[192,384]{1,0:T(8,128)(2,1)}, u32[]{:S(2)}, u32[]{:S(2)}) collective-permute-start(bf16[192,384]{1,0:T(8,128)(2,1)} %get-tuple-element.154), channel_id=1, source_target_pairs={{0,7},{1,6},{2,5},{3,4},{4,3},{5,2},{6,1},{7,0},{8,15},{9,14},{10,... | collective-permute-start | bytes 442376 | tf_op jit(solution)/shard_map/cond/branch_2_fun/ppermute | solution.py:292
where the time goes:
time: 187 us; the launch traced here: 186 us
  waiting for transfers between devices  97 us (52%)
  starting transfers between devices  44.9 us (24%)
  Pallas kernels  37.5 us (20%)
  local copies, waits for them, and re-layouts  4.82 us (3%)
    ppermute x9, waiting for transfers between devices, down(): lax.ppermute(window, 'loader', [(i, i - group) for i in range(group, devi...  66.2 us
    all_to_all x5, starting transfers between devices, exchange(): lax.all_to_all(parts, 'loader', 0, 0, axis_index_groups=planes, tiled=True)  19.5 us
    ppermute x7, waiting for transfers between devices, exchange_apart(): lax.ppermute(parts[k], 'loader', [(i, i ^ k) for i in range(devices)])  13.1 us
    all_to_all x5, waiting for transfers between devices, exchange(): lax.all_to_all(parts, 'loader', 0, 0, axis_index_groups=planes, tiled=True)  12 us
    ppermute x9, starting transfers between devices, down(): lax.ppermute(window, 'loader', [(i, i - group) for i in range(group, devi...  11.6 us
    pallas_call x2, Pallas kernels, assemble(): pl.pallas_call(assemble_kernel, out_shape=jax.ShapeDtypeStruct((rows, par...  7.64 us
    pallas_call x3, Pallas kernels, window_of(): pl.pallas_call(window_kernel, out_shape=jax.ShapeDtypeStruct((length, par...  7.63 us
    all_to_all x1, starting transfers between devices, all_counts_of(): return lax.all_to_all(counts, 'loader', 0, 0, tiled=True)  7.33 us
  transfers between devices with their start and end apart: 22, of which 15 were waited for; matrix products, arithmetic and copies ran while one was open for 1% of the time, Pallas kernels for 13%

commit v1 on v0

--- a/solution.py
+++ b/solution.py
@@ -210,35 +210,52 @@
     place_window(edges, apart_ref[0], group, target.shape[0], window, target)
 
 
-def finish_kernel(apart, *rest):
-    parts, (packed, scores) = rest[:-2], rest[-2:]
-    group = packed.shape[0] // (parts[0].shape[-2])
+def unit_of(values, dtype):
+    values = values.astype(jnp.float32)
+    scale = lax.rsqrt(jnp.sum(values * values, axis=1, keepdims=True) / values.shape[1] + epsilon)
+    return (values * scale).astype(dtype)
+
+
+def stage_kernel(apart, width, *rest):
+    parts, staged = rest[:-1], rest[-1]
+    group = staged.shape[0] // parts[0].shape[-2]
     member = lax.axis_index("loader") % group
-    turn, width = group * TILE, packed.shape[1] // 2
-    r = lax.broadcasted_iota(jnp.int32, (turn, turn), 0)
-    c = lax.broadcasted_iota(jnp.int32, (turn, turn), 1)
+    turn = group * TILE
 
     def step(t, _):
         source = pl.ds(pl.multiple_of(t * TILE, TILE), TILE)
         column, index = 0, 0
-        for split in apart:
+        for split in apart[:-1]:
             width_here = parts[index].shape[-1]
             for k in range(group):
                 owner = jnp.bitwise_xor(member, k) if split else k
                 at = pl.ds(pl.multiple_of(t * turn + owner * TILE, TILE), TILE)
                 tile = parts[index + k][source, :] if split else parts[index][k, source, :]
-                packed[at, column : column + width_here] = tile
+                staged[at, column : column + width_here] = tile
             column += width_here
             index += group if split else 1
         rows = pl.ds(pl.multiple_of(t * turn, turn), turn)
-        units = []
-        for low in (0, width):
-            values = packed[rows, low : low + width].astype(jnp.float32)
-            scale = lax.rsqrt(jnp.sum(values * values, axis=1, keepdims=True) / width + epsilon)
-            unit = (values * scale).astype(packed.dtype)
-            packed[rows, low : low + width] = unit
-            units.append(unit)
-        products = lax.dot_general(*units, (((1,), (1,)), ((), ())), preferred_element_type=jnp.float32)
+        staged[rows, :width] = unit_of(staged[rows, :width], staged.dtype)
+        return 0
+
+    lax.fori_loop(0, staged.shape[0] // turn, step, 0, unroll=2)
+
+
+def finish_kernel(staged, last, packed, scores):
+    group, width = last.shape[0], packed.shape[1] // 2
+    turn = group * TILE
+    r = lax.broadcasted_iota(jnp.int32, (turn, turn), 0)
+    c = lax.broadcasted_iota(jnp.int32, (turn, turn), 1)
+
+    def step(t, _):
+        source = pl.ds(pl.multiple_of(t * TILE, TILE), TILE)
+        rows = pl.ds(pl.multiple_of(t * turn, turn), turn)
+        tiles = jnp.concatenate([last[owner, source, :] for owner in range(group)], axis=0)
+        right = unit_of(jnp.concatenate([staged[rows, width:], tiles], axis=1), packed.dtype)
+        left = staged[rows, :width]
+        packed[rows, :width] = left
+        packed[rows, width:] = right
+        products = lax.dot_general(left, right, (((1,), (1,)), ((), ())), preferred_element_type=jnp.float32)
         own = jnp.where(r == c, products, 0.0)
         scores[pl.ds(t, 1), :] = jnp.sum(own, axis=0, keepdims=True) / width
         return 0
@@ -386,8 +403,9 @@
                     window = down(window[:length])
                     windows.append(window)
                 held = (assemble_apart if APART[chunk] else assemble)(chunks[chunk], windows)
+                if chunk + 1 == len(widths):
+                    return done, held
                 done += exchange_apart(held, devices) if APART[chunk] else [gather(held)]
-            return done
 
         return run
 
@@ -409,17 +427,17 @@
             return window, held
 
         _, held = lax.fori_loop(1, planes, hop, (window, held))
-        held = gather(held)
+        early = gather(held[:, : bounds[-2]])
         member = lax.axis_index("loader") % group
         done = []
-        for split, low, high in zip(APART, bounds, bounds[1:]):
+        for split, low, high in zip(APART, bounds, bounds[1:-1]):
             if split:
                 done += [
-                    lax.dynamic_index_in_dim(held, member ^ k, 0, keepdims=False)[:, low:high] for k in range(group)
+                    lax.dynamic_index_in_dim(early, member ^ k, 0, keepdims=False)[:, low:high] for k in range(group)
                 ]
             else:
-                done.append(held[:, :, low:high])
-        return done
+                done.append(early[:, :, low:high])
+        return done, held[:, bounds[-2] :]
 
     lengths = [w for w in WINDOWS if w[0] <= rows and len(w) < planes]
     chosen = pl.pallas_call(
@@ -431,17 +449,26 @@
     )(edges)
     received = exchange(first, devices)
     branches = [fixed(w) for w in lengths] + [general]
-    done = lax.switch(chosen[0], branches, received, pack_rest())
+    done, held = lax.switch(chosen[0], branches, received, pack_rest())
+    last = gather(held)
+    staged = pl.pallas_call(
+        functools.partial(stage_kernel, APART, width),
+        out_shape=jax.ShapeDtypeStruct((rows, bounds[-2]), dtype),
+        in_specs=[VMEM] * len(done),
+        out_specs=VMEM,
+        cost_estimate=pl.CostEstimate(flops=2**31, bytes_accessed=8 * rows * width, transcendentals=rows),
+        name="stage",
+    )(*done)
     packed_pairs, scores = pl.pallas_call(
-        functools.partial(finish_kernel, APART),
+        finish_kernel,
         out_shape=[
             jax.ShapeDtypeStruct((rows, 2 * width), dtype),
             jax.ShapeDtypeStruct((rows // turn, turn), jnp.float32),
         ],
-        in_specs=[VMEM] * len(done),
+        in_specs=[VMEM] * 2,
         out_specs=[VMEM] * 2,
         name="finish",
-    )(*done)
+    )(staged, last)
     return packed_pairs, scores.reshape(rows)
 
 

time: 187 us -> 192 us (1.027)
  Pallas kernels: 37.5 us -> 41.4 us
    ppermute x7, waiting for transfers between devices: 13.1 us -> 6.79 us  [exchange_apart(): lax.ppermute(parts[k], 'loader', [(i, i ^ k) for i in range(devices)])]
    all_to_all x5, waiting for transfers between devices: 12 us -> 17.7 us  [exchange(): lax.all_to_all(parts, 'loader', 0, 0, axis_index_groups=planes, tiled=True)]
    pallas_call x1 -> x2, Pallas kernels: 6.51 us -> 10.3 us  [the longest x1 5.62 us: shards(): pl.pallas_call(finish_kernel, out_shape=[jax.ShapeDtypeStruct((rows, 2 *...]
  transfers between devices with their start and end apart: 22 -> 22, of which waited for: 15 -> 12; matrix products, arithmetic and copies ran while one was open for 1% -> 1% of each run, Pallas kernels for 13% -> 15%
where the time goes in v1:
time: 192 us; the launch traced here: 191 us
  waiting for transfers between devices  97.6 us (51%)
  starting transfers between devices  43.8 us (23%)
  Pallas kernels  41.4 us (22%)
  local copies, waits for them, and re-layouts  5.68 us (3%)
    ppermute x9, waiting for transfers between devices, down(): lax.ppermute(window, 'loader', [(i, i - group) for i in range(group, devi...  67.3 us
    all_to_all x5, starting transfers between devices, exchange(): lax.all_to_all(parts, 'loader', 0, 0, axis_index_groups=planes, tiled=True)  19 us
    all_to_all x5, waiting for transfers between devices, exchange(): lax.all_to_all(parts, 'loader', 0, 0, axis_index_groups=planes, tiled=True)  17.7 us
    ppermute x9, starting transfers between devices, down(): lax.ppermute(window, 'loader', [(i, i - group) for i in range(group, devi...  11.6 us
    pallas_call x2, Pallas kernels, assemble(): pl.pallas_call(assemble_kernel, out_shape=jax.ShapeDtypeStruct((rows, par...  7.63 us
    pallas_call x3, Pallas kernels, window_of(): pl.pallas_call(window_kernel, out_shape=jax.ShapeDtypeStruct((length, par...  7.63 us
    all_to_all x1, starting transfers between devices, all_counts_of(): return lax.all_to_all(counts, 'loader', 0, 0, tiled=True)  7.33 us
    ppermute x7, waiting for transfers between devices, exchange_apart(): lax.ppermute(parts[k], 'loader', [(i, i ^ k) for i in range(devices)])  6.79 us
  transfers between devices with their start and end apart: 22, of which 12 were waited for; matrix products, arithmetic and copies ran while one was open for 1% of the time, Pallas kernels for 15%

profile of v1, /device:TPU:0, one launch (start us, length us, event | category | flops | bytes accessed | tf_op | source)
XLA Modules:
  0.0 190.6 jit_solution(5938096439130389771)
XLA Ops:
  0.6 1.4 count.1
  2.1 7.3 %all-to-all-start.15 = ((s32[32,1,128]{2,1,0:T(1,128)}), s32[32,1,128]{2,1,0:T(1,128)S(1)}, u32[]{:S(2)}, u32[]{:S(2)}) async-start(s32[32,1,128]{2,1,0:T(1,128)} %bitcast.37), calls=%async_computation.15 | async-start | bytes 32768 | tf_op jit(solution)/shard_map/all_to_all | solution.py:297
  10.7 5.8 %all-to-all-done.15 = s32[32,1,128]{2,1,0:T(1,128)S(1)} async-done(((s32[32,1,128]{2,1,0:T(1,128)}), s32[32,1,128]{2,1,0:T(1,128)S(1)}, u32[]{:S(2)}, u32[]{:S(2)}) %all-to-all-start.15) | async-done | bytes 16416 | tf_op jit(solution)/shard_map/all_to_all | solution.py:297
  17.1 3.7 %pack_first.1 = (bf16[8,192,384]{2,1,0:T(8,128)(2,1)}, s32[33]{0:T(128)S(1)}) custom-call(s32[32,128]{1,0:T(8,128)} %bitcast.36, s32[6]{0:T(128)} %reduce_sum.9.sums_ref, s32[6,256]{1,0:T(8,128)} %copy-done.23, bf16[1536,512]{1,0:T(8,128)(2,1)} %left_ref.1), custom_call_target="tpu_custom_call" | custom-call | tf_op jit(solution)/shard_map/pack_first/pallas_call | solution.py:334
  20.8 3.6 %all-to-all-start.16 = ((bf16[8,192,384]{2,1,0:T(8,128)(2,1)}), bf16[8,192,384]{2,1,0:T(8,128)(2,1)S(1)}, u32[]{:S(2)}, u32[]{:S(2)}) async-start(bf16[8,192,384]{2,1,0:T(8,128)(2,1)} %get-tuple-element.201), calls=%async_computation.16 | async-start | bytes 2359296 | tf_op jit(solution)/shard_map/all_to_all | solution.py:303
  24.4 1.1 choose.1
  26.1 5.1 %pack_rest.1 = (bf16[8,192,384]{2,1,0:T(8,128)(2,1)}, bf16[8,192,256]{2,1,0:T(8,128)(2,1)}) custom-call(s32[33]{0:T(128)S(1)} %get-tuple-element.200.edges, s32[6]{0:T(128)} %reduce_sum.9.sums_ref, s32[6,256]{1,0:T(8,128)} %copy-done.23, bf16[1536,512]{1,0:T(8,128)(2,1)} %left_ref.1, bf16[1536,512]{1,0:T(8,128)(2,1)} %right_ref.1), custom_call_target="tpu_custom_call" | custom-call | flops 2147483648 | bytes 6291456 | tf_op jit(solution)/shard_map/pack_rest/pallas_call | solution.py:345
  31.2 9.8 %all-to-all-done.16 = bf16[8,192,384]{2,1,0:T(8,128)(2,1)S(1)} async-done(((bf16[8,192,384]{2,1,0:T(8,128)(2,1)}), bf16[8,192,384]{2,1,0:T(8,128)(2,1)S(1)}, u32[]{:S(2)}, u32[]{:S(2)}) %all-to-all-start.16) | async-done | bytes 1179680 | tf_op jit(solution)/shard_map/all_to_all | solution.py:303
  41.1 126.8 %conditional.1 = (bf16[8,192,384]{2,1,0:T(8,128)(2,1)}, bf16[192,384]{1,0:T(8,128)(2,1)}, bf16[192,384]{1,0:T(8,128)(2,1)}, bf16[192,384]{1,0:T(8,128)(2,1)}, bf...) conditional(s32[]{:T(128)} %bitcast.17, (s32[33]{0:T(128)S(1)}, ...), branch_computations={%region_1.0_spmd, %region_2.0_spmd, %region_3.0_spmd, %region_4.0_... | conditional | flops 6442450944 | bytes 98632608 | solution.py:452
  41.1 2.1 %window.19 = bf16[768,384]{1,0:T(8,128)(2,1)} custom-call(s32[33]{0:T(128)S(1)} %get-tuple-element.140.edges, bf16[8,192,384]{2,1,0:T(8,128)(2,1)S(1)} %get-tuple-element.141.parts), custom_call_target="tpu_custom_call" | custom-call | flops 1073741824 | bytes 1572864 | tf_op jit(solution)/shard_map/cond/branch_2_fun/window/pallas_call | solution.py:356
  43.2 3.7 %all-to-all-start.7 = ((bf16[8,192,384]{2,1,0:T(8,128)(2,1)}), bf16[8,192,384]{2,1,0:T(8,128)(2,1)S(1)}, u32[]{:S(2)}, u32[]{:S(2)}) async-start(bf16[8,192,384]{2,1,0:T(8,128)(2,1)} %get-tuple-element.144), calls=%async_computation.7 | async-start | bytes 2359296 | tf_op jit(solution)/shard_map/cond/branch_2_fun/all_to_all | solution.py:303
  46.9 1.3 collective-permute-start.26
  48.2 16.2 %collective-permute-done.26.rest_0_ = bf16[768,384]{1,0:T(8,128)(2,1)S(1)} collective-permute-done((bf16[768,384]{1,0:T(8,128)(2,1)S(1)}, bf16[768,384]{1,0:T(8,128)(2,1)S(1)}, u32[]{:S(2)}, u32[]{:S(2)}) %collective-permute-start.26) | collective-permute-done | bytes 589856 | tf_op jit(solution)/shard_map/cond/branch_2_fun/ppermute | solution.py:387
  64.4 1.3 collective-permute-start.27
  65.7 1.0 copy-done.6
  66.8 2.9 %window.20 = bf16[768,384]{1,0:T(8,128)(2,1)} custom-call(s32[33]{0:T(128)S(1)} %get-tuple-element.140.edges, bf16[8,192,384]{2,1,0:T(8,128)(2,1)} %copy-done.6), custom_call_target="tpu_custom_call" | custom-call | flops 1073741824 | bytes 1572864 | tf_op jit(solution)/shard_map/cond/branch_2_fun/window/pallas_call | solution.py:356
  69.6 3.9 %all-to-all-start.8 = ((bf16[8,192,256]{2,1,0:T(8,128)(2,1)}), bf16[8,192,256]{2,1,0:T(8,128)(2,1)S(1)}, u32[]{:S(2)}, u32[]{:S(2)}) async-start(bf16[8,192,256]{2,1,0:T(8,128)(2,1)} %get-tuple-element.155), calls=%async_computation.8 | async-start | bytes 1572864 | tf_op jit(solution)/shard_map/cond/branch_2_fun/all_to_all | solution.py:303
  73.5 1.3 collective-permute-start.29
  74.8 7.7 %collective-permute-done.27.rest_1_ = bf16[768,384]{1,0:T(8,128)(2,1)S(1)} collective-permute-done((bf16[768,384]{1,0:T(8,128)(2,1)S(1)}, bf16[768,384]{1,0:T(8,128)(2,1)S(1)}, u32[]{:S(2)}, u32[]{:S(2)}) %collective-permute-start.27) | collective-permute-done | bytes 589856 | tf_op jit(solution)/shard_map/cond/branch_2_fun/ppermute | solution.py:387
  82.5 1.3 collective-permute-start.28
  83.8 11.4 %collective-permute-done.29.rest_0_ = bf16[768,384]{1,0:T(8,128)(2,1)} collective-permute-done((bf16[768,384]{1,0:T(8,128)(2,1)}, bf16[768,384]{1,0:T(8,128)(2,1)}, u32[]{:S(2)}, u32[]{:S(2)}) %collective-permute-start.29) | collective-permute-done | bytes 589856 | tf_op jit(solution)/shard_map/cond/branch_2_fun/ppermute | solution.py:387
  95.2 1.3 collective-permute-start.30
  96.5 0.9 copy-done.10
  97.4 2.6 %window.21 = bf16[768,256]{1,0:T(8,128)(2,1)} custom-call(s32[33]{0:T(128)S(1)} %get-tuple-element.140.edges, bf16[8,192,256]{2,1,0:T(8,128)(2,1)} %copy-done.10), custom_call_target="tpu_custom_call" | custom-call | flops 1073741824 | bytes 1572864 | tf_op jit(solution)/shard_map/cond/branch_2_fun/window/pallas_call | solution.py:356
  100.1 1.3 collective-permute-start.39
  101.3 2.3 %collective-permute-done.28.rest_2_ = bf16[512,384]{1,0:T(8,128)(2,1)} collective-permute-done((bf16[512,384]{1,0:T(8,128)(2,1)S(1)}, bf16[512,384]{1,0:T(8,128)(2,1)}, u32[]{:S(2)}, u32[]{:S(2)}) %collective-permute-start.28) | collective-permute-done | bytes 393248 | tf_op jit(solution)/shard_map/cond/branch_2_fun/ppermute | solution.py:387
  103.6 3.9 %assemble.13 = bf16[1536,384]{1,0:T(8,128)(2,1)} custom-call(s32[33]{0:T(128)S(1)} %get-tuple-element.140.edges, bf16[8,192,384]{2,1,0:T(8,128)(2,1)S(1)} %get-tuple-element.141.parts, bf16[768,384]{1,0:T(8,128)(2,1)} %copy-done.29, bf16[768,384]{1,0:T(8,128)(2,1)} %copy-done.20, bf16[512,384]{1,0:T(8,128)(2,1)} %collective-permute-done.28.rest_2_), custom_call_target="tpu_custom_call" | custom-call | flops 1073741824 | bytes 3145728 | tf_op jit(solution)/shard_map/cond/branch_2_fun/assemble/pallas_call | solution.py:366
  107.5 4.3 %all-to-all-start.6 = ((bf16[8,192,384]{2,1,0:T(8,128)(2,1)}), bf16[8,192,384]{2,1,0:T(8,128)(2,1)}, u32[]{:S(2)}, u32[]{:S(2)}) async-start(bf16[8,192,384]{2,1,0:T(8,128)(2,1)} %bitcast.35), calls=%async_computation.6 | async-start | bytes 2359296 | tf_op jit(solution)/shard_map/cond/branch_2_fun/all_to_all | solution.py:303
  111.8 11.4 %collective-permute-done.39.rest_0_ = bf16[768,256]{1,0:T(8,128)(2,1)S(1)} collective-permute-done((bf16[768,256]{1,0:T(8,128)(2,1)}, bf16[768,256]{1,0:T(8,128)(2,1)S(1)}, u32[]{:S(2)}, u32[]{:S(2)}) %collective-permute-start.39) | collective-permute-done | bytes 393248 | tf_op jit(solution)/shard_map/cond/branch_2_fun/ppermute | solution.py:387
  123.2 1.3 collective-permute-start.40
  124.6 1.3 collective-permute-start.31
  125.9 11.2 %collective-permute-done.40.rest_1_ = bf16[768,256]{1,0:T(8,128)(2,1)S(1)} collective-permute-done((bf16[768,256]{1,0:T(8,128)(2,1)S(1)}, bf16[768,256]{1,0:T(8,128)(2,1)S(1)}, u32[]{:S(2)}, u32[]{:S(2)}) %collective-permute-start.40) | collective-permute-done | bytes 393248 | tf_op jit(solution)/shard_map/cond/branch_2_fun/ppermute | solution.py:387
  137.1 1.3 collective-permute-start.41
  138.4 7.1 %collective-permute-done.31.rest_2_ = bf16[512,384]{1,0:T(8,128)(2,1)S(1)} collective-permute-done((bf16[512,384]{1,0:T(8,128)(2,1)S(1)}, bf16[512,384]{1,0:T(8,128)(2,1)S(1)}, u32[]{:S(2)}, u32[]{:S(2)}) %collective-permute-start.31) | collective-permute-done | bytes 393248 | tf_op jit(solution)/shard_map/cond/branch_2_fun/ppermute | solution.py:387
  145.5 0.7 copy-done.35
  146.3 4.4 %assemble_apart.6 = (bf16[192,384]{1,0:T(8,128)(2,1)}, bf16[192,384]{1,0:T(8,128)(2,1)}, bf16[192,384]{1,0:T(8,128)(2,1)}, bf16[192,384]{1,0:T(8,128)(2,1)}, bf1...) custom-call(s32[33]{0:T(128)S(1)} %get-tuple-element.140.edges, ...), custom_call_target="tpu_custom_call" | custom-call | flops 1073741824 | bytes 3145728 | tf_op jit(solution)/shard_map/cond/branch_2_fun/assemble_apart/pallas_call | solution.py:376
  150.7 1.4 collective-permute-start.33
  152.6 1.4 collective-permute-start.35
  154.3 3.5 %collective-permute-done.33 = bf16[192,384]{1,0:T(8,128)(2,1)} collective-permute-done((bf16[192,384]{1,0:T(8,128)(2,1)}, bf16[192,384]{1,0:T(8,128)(2,1)}, u32[]{:S(2)}, u32[]{:S(2)}) %collective-permute-start.33) | collective-permute-done | bytes 147488 | tf_op jit(solution)/shard_map/cond/branch_2_fun/ppermute | solution.py:309
  157.8 2.3 %collective-permute-start.37 = (bf16[192,384]{1,0:T(8,128)(2,1)}, bf16[192,384]{1,0:T(8,128)(2,1)}, u32[]{:S(2)}, u32[]{:S(2)}) collective-permute-start(bf16[192,384]{1,0:T(8,128)(2,1)} %get-tuple-element.153), channel_id=1, source_target_pairs={{0,6},{1,7},{2,4},{3,5},{4,2},{5,3},{6,0},{7,1},{8,14},{9,15},{10,... | collective-permute-start | bytes 442376 | tf_op jit(solution)/shard_map/cond/branch_2_fun/ppermute | solution.py:309
  160.2 0.7 copy-done.37
  160.9 3.7 %assemble.14 = bf16[1536,256]{1,0:T(8,128)(2,1)} custom-call(s32[33]{0:T(128)S(1)} %get-tuple-element.140.edges, bf16[8,192,256]{2,1,0:T(8,128)(2,1)} %copy-done.10, bf16[768,256]{1,0:T(8,128)(2,1)} %copy-done.34, bf16[768,256]{1,0:T(8,128)(2,1)} %copy-done.22, bf16[512,256]{1,0:T(8,128)(2,1)} %copy-done.37), custom_call_target="tpu_custom_call" | custom-call | flops 1073741824 | bytes 3145728 | tf_op jit(solution)/shard_map/cond/branch_2_fun/assemble/pallas_call | solution.py:366
  164.6 3.2 %collective-permute-done.36 = bf16[192,384]{1,0:T(8,128)(2,1)} collective-permute-done((bf16[192,384]{1,0:T(8,128)(2,1)}, bf16[192,384]{1,0:T(8,128)(2,1)}, u32[]{:S(2)}, u32[]{:S(2)}) %collective-permute-start.36) | collective-permute-done | bytes 147488 | tf_op jit(solution)/shard_map/cond/branch_2_fun/ppermute | solution.py:309
  167.9 3.6 %all-to-all-start.17 = ((bf16[8,192,256]{2,1,0:T(8,128)(2,1)}), bf16[8,192,256]{2,1,0:T(8,128)(2,1)S(1)}, u32[]{:S(2)}, u32[]{:S(2)}) async-start(bf16[8,192,256]{2,1,0:T(8,128)(2,1)} %bitcast.18), calls=%async_computation.17 | async-start | bytes 1572864 | tf_op jit(solution)/shard_map/all_to_all | solution.py:303
  171.5 4.7 %stage.1.staged = bf16[1536,768]{1,0:T(8,128)(2,1)} custom-call(bf16[8,192,384]{2,1,0:T(8,128)(2,1)} %get-tuple-element.204.rest_0_, bf16[192,384]{1,0:T(8,128)(2,1)} %get-tuple-element.205.rest_1_, bf16[192,384]{1,0:T(8,128)(2,1)} %get-tuple-element.206.rest_2_, bf16[192,384]{1,0:T(8,128)(2,1)} %get-tuple-element.207.rest_3_, ...), custom_call_target="tpu_custom_call" | custom-call | flops 2147483648 | bytes 6291456 | tf_op jit(solution)/shard_map/stage/pallas_call | solution.py:454
  176.2 7.9 %all-to-all-done.17.last = bf16[8,192,256]{2,1,0:T(8,128)(2,1)S(1)} async-done(((bf16[8,192,256]{2,1,0:T(8,128)(2,1)}), bf16[8,192,256]{2,1,0:T(8,128)(2,1)S(1)}, u32[]{:S(2)}, u32[]{:S(2)}) %all-to-all-start.17) | async-done | bytes 786464 | tf_op jit(solution)/shard_map/all_to_all | solution.py:303
  184.1 0.9 copy-done.4
  185.0 5.6 %finish.1 = (bf16[1536,1024]{1,0:T(8,128)(2,1)}, f32[12,128]{1,0:T(8,128)}) custom-call(bf16[1536,768]{1,0:T(8,128)(2,1)} %stage.1.staged, bf16[8,192,256]{2,1,0:T(8,128)(2,1)} %copy-done.4), custom_call_target="tpu_custom_call" | custom-call | tf_op jit(solution)/shard_map/finish/pallas_call | solution.py:462
  (40 shorter events, 2.8 us)
Async XLA Ops:
  2.1 14.4 %all-to-all-start.15 = ((s32[32,1,128]{2,1,0:T(1,128)}), s32[32,1,128]{2,1,0:T(1,128)S(1)}, u32[]{:S(2)}, u32[]{:S(2)}) async-start(s32[32,1,128]{2,1,0:T(1,128)} %bitcast.37), calls=%async_computation.15 | async-start | bytes 32768 | tf_op jit(solution)/shard_map/all_to_all | solution.py:297
  10.1 6.4 %copy-start.23 = (s32[6,256]{1,0:T(8,128)}, s32[6,256]{1,0:T(8,128)S(1)}, u32[]{:S(2)}) copy-start(s32[6,256]{1,0:T(8,128)S(1)} %reshape.36.marks_ref) | copy-start | bytes 18436
  16.5 0.6 copy-start.24
  20.8 20.3 %all-to-all-start.16 = ((bf16[8,192,384]{2,1,0:T(8,128)(2,1)}), bf16[8,192,384]{2,1,0:T(8,128)(2,1)S(1)}, u32[]{:S(2)}, u32[]{:S(2)}) async-start(bf16[8,192,384]{2,1,0:T(8,128)(2,1)} %get-tuple-element.201), calls=%async_computation.16 | async-start | bytes 2359296 | tf_op jit(solution)/shard_map/all_to_all | solution.py:303
  43.2 3.7 %copy-start.30 = (bf16[768,384]{1,0:T(8,128)(2,1)S(1)}, bf16[768,384]{1,0:T(8,128)(2,1)}, u32[]{:S(2)}) copy-start(bf16[768,384]{1,0:T(8,128)(2,1)} %window.19) | copy-start | bytes 1769476 | tf_op jit(solution)/shard_map/cond
  43.2 22.5 %all-to-all-start.7 = ((bf16[8,192,384]{2,1,0:T(8,128)(2,1)}), bf16[8,192,384]{2,1,0:T(8,128)(2,1)S(1)}, u32[]{:S(2)}, u32[]{:S(2)}) async-start(bf16[8,192,384]{2,1,0:T(8,128)(2,1)} %get-tuple-element.144), calls=%async_computation.7 | async-start | bytes 2359296 | tf_op jit(solution)/shard_map/cond/branch_2_fun/all_to_all | solution.py:303
  46.9 17.5 %collective-permute-start.26 = (bf16[768,384]{1,0:T(8,128)(2,1)S(1)}, bf16[768,384]{1,0:T(8,128)(2,1)S(1)}, u32[]{:S(2)}, u32[]{:S(2)}) collective-permute-start(bf16[768,384]{1,0:T(8,128)(2,1)S(1)} %copy-done.30), channel_id=1, source_target_pairs={{8,0},{9,1},{10,2},{11,3},{12,4},{13,5},{14,6},{15,7},{16,8},{17,9... | collective-permute-start | bytes 1769480 | tf_op jit(solution)/shard_map/cond/branch_2_fun/ppermute | solution.py:387
  64.4 19.4 %copy-start.29 = (bf16[768,384]{1,0:T(8,128)(2,1)}, bf16[768,384]{1,0:T(8,128)(2,1)S(1)}, u32[]{:S(2)}) copy-start(bf16[768,384]{1,0:T(8,128)(2,1)S(1)} %collective-permute-done.26.rest_0_) | copy-start | bytes 1769476 | tf_op jit(solution)/shard_map/cond
  64.4 18.0 %collective-permute-start.27 = (bf16[768,384]{1,0:T(8,128)(2,1)S(1)}, bf16[768,384]{1,0:T(8,128)(2,1)S(1)}, u32[]{:S(2)}, u32[]{:S(2)}) collective-permute-start(bf16[768,384]{1,0:T(8,128)(2,1)S(1)} %collective-permute-done.26.rest_0_), channel_id=1, source_target_pairs={{8,0},{9,1},{10,2},{11,3},{12,4},{13,5},{14,6},{15,7},{16,8},{17,9... | collective-permute-start | bytes 1769480 | tf_op jit(solution)/shard_map/cond/branch_2_fun/ppermute | solution.py:387
  65.7 1.0 copy-start.6
  69.6 26.9 %all-to-all-start.8 = ((bf16[8,192,256]{2,1,0:T(8,128)(2,1)}), bf16[8,192,256]{2,1,0:T(8,128)(2,1)S(1)}, u32[]{:S(2)}, u32[]{:S(2)}) async-start(bf16[8,192,256]{2,1,0:T(8,128)(2,1)} %get-tuple-element.155), calls=%async_computation.8 | async-start | bytes 1572864 | tf_op jit(solution)/shard_map/cond/branch_2_fun/all_to_all | solution.py:303
  73.5 21.7 %collective-permute-start.29 = (bf16[768,384]{1,0:T(8,128)(2,1)}, bf16[768,384]{1,0:T(8,128)(2,1)}, u32[]{:S(2)}, u32[]{:S(2)}) collective-permute-start(bf16[768,384]{1,0:T(8,128)(2,1)} %window.20), channel_id=1, source_target_pairs={{8,0},{9,1},{10,2},{11,3},{12,4},{13,5},{14,6},{15,7},{16,8},{17,9... | collective-permute-start | bytes 1769480 | tf_op jit(solution)/shard_map/cond/branch_2_fun/ppermute | solution.py:387
  82.5 17.6 %copy-start.20 = (bf16[768,384]{1,0:T(8,128)(2,1)}, bf16[768,384]{1,0:T(8,128)(2,1)S(1)}, u32[]{:S(2)}) copy-start(bf16[768,384]{1,0:T(8,128)(2,1)S(1)} %collective-permute-done.27.rest_1_) | copy-start | bytes 1769476 | tf_op jit(solution)/shard_map/cond
  82.5 21.1 %collective-permute-start.28 = (bf16[512,384]{1,0:T(8,128)(2,1)S(1)}, bf16[512,384]{1,0:T(8,128)(2,1)}, u32[]{:S(2)}, u32[]{:S(2)}) collective-permute-start(bf16[512,384]{1,0:T(8,128)(2,1)S(1)} %slice.75), channel_id=1, source_target_pairs={{8,0},{9,1},{10,2},{11,3},{12,4},{13,5},{14,6},{15,7},{16,8},{17,9... | collective-permute-start | bytes 1179656 | tf_op jit(solution)/shard_map/cond/branch_2_fun/ppermute | solution.py:387
  95.2 29.3 %collective-permute-start.30 = (bf16[768,384]{1,0:T(8,128)(2,1)}, bf16[768,384]{1,0:T(8,128)(2,1)S(1)}, u32[]{:S(2)}, u32[]{:S(2)}) collective-permute-start(bf16[768,384]{1,0:T(8,128)(2,1)} %collective-permute-done.29.rest_0_), channel_id=1, source_target_pairs={{8,0},{9,1},{10,2},{11,3},{12,4},{13,5},{14,6},{15,7},{16,8},{17,9... | collective-permute-start | bytes 1769480 | tf_op jit(solution)/shard_map/cond/branch_2_fun/ppermute | solution.py:387
  96.5 0.9 copy-start.10
  100.1 23.2 %collective-permute-start.39 = (bf16[768,256]{1,0:T(8,128)(2,1)}, bf16[768,256]{1,0:T(8,128)(2,1)S(1)}, u32[]{:S(2)}, u32[]{:S(2)}) collective-permute-start(bf16[768,256]{1,0:T(8,128)(2,1)} %window.21), channel_id=1, source_target_pairs={{8,0},{9,1},{10,2},{11,3},{12,4},{13,5},{14,6},{15,7},{16,8},{17,9... | collective-permute-start | bytes 1179656 | tf_op jit(solution)/shard_map/cond/branch_2_fun/ppermute | solution.py:387
  107.5 57.1 %all-to-all-start.6 = ((bf16[8,192,384]{2,1,0:T(8,128)(2,1)}), bf16[8,192,384]{2,1,0:T(8,128)(2,1)}, u32[]{:S(2)}, u32[]{:S(2)}) async-start(bf16[8,192,384]{2,1,0:T(8,128)(2,1)} %bitcast.35), calls=%async_computation.6 | async-start | bytes 2359296 | tf_op jit(solution)/shard_map/cond/branch_2_fun/all_to_all | solution.py:303
  123.2 27.5 %copy-start.34 = (bf16[768,256]{1,0:T(8,128)(2,1)}, bf16[768,256]{1,0:T(8,128)(2,1)S(1)}, u32[]{:S(2)}) copy-start(bf16[768,256]{1,0:T(8,128)(2,1)S(1)} %collective-permute-done.39.rest_0_) | copy-start | bytes 1179652 | tf_op jit(solution)/shard_map/cond
  123.2 13.9 %collective-permute-start.40 = (bf16[768,256]{1,0:T(8,128)(2,1)S(1)}, bf16[768,256]{1,0:T(8,128)(2,1)S(1)}, u32[]{:S(2)}, u32[]{:S(2)}) collective-permute-start(bf16[768,256]{1,0:T(8,128)(2,1)S(1)} %collective-permute-done.39.rest_0_), channel_id=1, source_target_pairs={{8,0},{9,1},{10,2},{11,3},{12,4},{13,5},{14,6},{15,7},{16,8},{17,9... | collective-permute-start | bytes 1179656 | tf_op jit(solution)/shard_map/cond/branch_2_fun/ppermute | solution.py:387
  124.5 21.0 %copy-start.19 = (bf16[768,384]{1,0:T(8,128)(2,1)}, bf16[768,384]{1,0:T(8,128)(2,1)S(1)}, u32[]{:S(2)}) copy-start(bf16[768,384]{1,0:T(8,128)(2,1)S(1)} %collective-permute-done.30.rest_1_) | copy-start | bytes 1769476 | tf_op jit(solution)/shard_map/cond
  124.6 20.9 %collective-permute-start.31 = (bf16[512,384]{1,0:T(8,128)(2,1)S(1)}, bf16[512,384]{1,0:T(8,128)(2,1)S(1)}, u32[]{:S(2)}, u32[]{:S(2)}) collective-permute-start(bf16[512,384]{1,0:T(8,128)(2,1)S(1)} %slice.76), channel_id=1, source_target_pairs={{8,0},{9,1},{10,2},{11,3},{12,4},{13,5},{14,6},{15,7},{16,8},{17,9... | collective-permute-start | bytes 1179656 | tf_op jit(solution)/shard_map/cond/branch_2_fun/ppermute | solution.py:387
  137.1 23.1 %copy-start.22 = (bf16[768,256]{1,0:T(8,128)(2,1)}, bf16[768,256]{1,0:T(8,128)(2,1)S(1)}, u32[]{:S(2)}) copy-start(bf16[768,256]{1,0:T(8,128)(2,1)S(1)} %collective-permute-done.40.rest_1_) | copy-start | bytes 1179652 | tf_op jit(solution)/shard_map/cond
  137.1 23.0 %collective-permute-start.41 = (bf16[512,256]{1,0:T(8,128)(2,1)S(1)}, bf16[512,256]{1,0:T(8,128)(2,1)S(1)}, u32[]{:S(2)}, u32[]{:S(2)}) collective-permute-start(bf16[512,256]{1,0:T(8,128)(2,1)S(1)} %slice.77), channel_id=1, source_target_pairs={{8,0},{9,1},{10,2},{11,3},{12,4},{13,5},{14,6},{15,7},{16,8},{17,9... | collective-permute-start | bytes 786440 | tf_op jit(solution)/shard_map/cond/branch_2_fun/ppermute | solution.py:387
  145.5 0.8 copy-start.35
  150.7 3.3 %collective-permute-start.32 = (bf16[192,384]{1,0:T(8,128)(2,1)}, bf16[192,384]{1,0:T(8,128)(2,1)}, u32[]{:S(2)}, u32[]{:S(2)}) collective-permute-start(bf16[192,384]{1,0:T(8,128)(2,1)} %get-tuple-element.148), channel_id=1, source_target_pairs={{0,1},{1,0},{2,3},{3,2},{4,5},{5,4},{6,7},{7,6},{8,9},{9,8},{10,11... | collective-permute-start | bytes 442376 | tf_op jit(solution)/shard_map/cond/branch_2_fun/ppermute | solution.py:309
  150.7 7.1 %collective-permute-start.33 = (bf16[192,384]{1,0:T(8,128)(2,1)}, bf16[192,384]{1,0:T(8,128)(2,1)}, u32[]{:S(2)}, u32[]{:S(2)}) collective-permute-start(bf16[192,384]{1,0:T(8,128)(2,1)} %get-tuple-element.149), channel_id=1, source_target_pairs={{0,2},{1,3},{2,0},{3,1},{4,6},{5,7},{6,4},{7,5},{8,10},{9,11},{10,... | collective-permute-start | bytes 442376 | tf_op jit(solution)/shard_map/cond/branch_2_fun/ppermute | solution.py:309
  152.2 12.4 %collective-permute-start.34 = (bf16[192,384]{1,0:T(8,128)(2,1)}, bf16[192,384]{1,0:T(8,128)(2,1)}, u32[]{:S(2)}, u32[]{:S(2)}) collective-permute-start(bf16[192,384]{1,0:T(8,128)(2,1)} %get-tuple-element.150), channel_id=1, source_target_pairs={{0,3},{1,2},{2,1},{3,0},{4,7},{5,6},{6,5},{7,4},{8,11},{9,10},{10,... | collective-permute-start | bytes 442376 | tf_op jit(solution)/shard_map/cond/branch_2_fun/ppermute | solution.py:309
  152.6 12.1 %collective-permute-start.35 = (bf16[192,384]{1,0:T(8,128)(2,1)}, bf16[192,384]{1,0:T(8,128)(2,1)}, u32[]{:S(2)}, u32[]{:S(2)}) collective-permute-start(bf16[192,384]{1,0:T(8,128)(2,1)} %get-tuple-element.151), channel_id=1, source_target_pairs={{0,4},{1,5},{2,6},{3,7},{4,0},{5,1},{6,2},{7,3},{8,12},{9,13},{10,... | collective-permute-start | bytes 442376 | tf_op jit(solution)/shard_map/cond/branch_2_fun/ppermute | solution.py:309
  154.0 13.9 %collective-permute-start.36 = (bf16[192,384]{1,0:T(8,128)(2,1)}, bf16[192,384]{1,0:T(8,128)(2,1)}, u32[]{:S(2)}, u32[]{:S(2)}) collective-permute-start(bf16[192,384]{1,0:T(8,128)(2,1)} %get-tuple-element.152), channel_id=1, source_target_pairs={{0,5},{1,4},{2,7},{3,6},{4,1},{5,0},{6,3},{7,2},{8,13},{9,12},{10,... | collective-permute-start | bytes 442376 | tf_op jit(solution)/shard_map/cond/branch_2_fun/ppermute | solution.py:309
  157.8 10.0 %collective-permute-start.37 = (bf16[192,384]{1,0:T(8,128)(2,1)}, bf16[192,384]{1,0:T(8,128)(2,1)}, u32[]{:S(2)}, u32[]{:S(2)}) collective-permute-start(bf16[192,384]{1,0:T(8,128)(2,1)} %get-tuple-element.153), channel_id=1, source_target_pairs={{0,6},{1,7},{2,4},{3,5},{4,2},{5,3},{6,0},{7,1},{8,14},{9,15},{10,... | collective-permute-start | bytes 442376 | tf_op jit(solution)/shard_map/cond/branch_2_fun/ppermute | solution.py:309
  160.2 0.7 copy-start.37
  160.2 7.7 %collective-permute-start.38 = (bf16[192,384]{1,0:T(8,128)(2,1)}, bf16[192,384]{1,0:T(8,128)(2,1)}, u32[]{:S(2)}, u32[]{:S(2)}) collective-permute-start(bf16[192,384]{1,0:T(8,128)(2,1)} %get-tuple-element.154), channel_id=1, source_target_pairs={{0,7},{1,6},{2,5},{3,4},{4,3},{5,2},{6,1},{7,0},{8,15},{9,14},{10,... | collective-permute-start | bytes 442376 | tf_op jit(solution)/shard_map/cond/branch_2_fun/ppermute | solution.py:309
  167.9 16.2 %all-to-all-start.17 = ((bf16[8,192,256]{2,1,0:T(8,128)(2,1)}), bf16[8,192,256]{2,1,0:T(8,128)(2,1)S(1)}, u32[]{:S(2)}, u32[]{:S(2)}) async-start(bf16[8,192,256]{2,1,0:T(8,128)(2,1)} %bitcast.18), calls=%async_computation.17 | async-start | bytes 1572864 | tf_op jit(solution)/shard_map/all_to_all | solution.py:303
  184.1 0.9 copy-start.4
